TPU v7x, 256 devices: a whole 4x4x8 slice. The times are simulated.
256 devices in a mesh: row: 16 (over z_hi, x, core), col: 16 (over y, z_lo).
Axes of the slice: x: 4, y: 4, z: 8 (z_hi: 2, z_lo: 4; z = z_hi * 4 + z_lo), core: 2. Of those that a mesh axis runs over, the one named last changes fastest.
Arguments:
- covariance: float32 [16384, 16384], P('row', 'col'), may hold values from -10 to 14, as said below
- wind_x: float32 [128, 128], replicated, may hold values from -0.2 to 0.2
- wind_y: float32 [128, 128], replicated, may hold values from -0.2 to 0.2
- patch_map: int32 [128, 128], replicated, may hold values from 0 to 15
- kappa_table: float32 [16], replicated, may hold values from 0.1 to 0.24
Outputs:
- forecast: float32 [16384, 16384], P('row', 'col')
Inputs may be any that keep to these rules, and one draw needn't show every extreme that they name: covariance is symmetric.
All inputs are finite; a program needn't handle non-finite values.
Results may differ from a plain program's by a relative error of at most 0.00002.
Values sent between devices are 32-bit elements; how exact they have to be, the bound alone decides.
A program may use at most 64 MiB of HBM per device.

v0:
```python
import jax
import jax.numpy as jnp
from jax import lax
from jax.sharding import PartitionSpec as P

GY = 128
SUBSTEPS = 4
PATCHES = 16


def with_halo(cells, sides, width):
    for axis, dim in sides:
        count = lax.axis_size(axis)
        ends = count - 1
        head = lax.slice_in_dim(cells, 0, width, axis=dim)
        tail = lax.slice_in_dim(cells, cells.shape[dim] - width, cells.shape[dim], axis=dim)
        cells = jnp.concatenate(
            [
                lax.ppermute(tail, axis, [(i, (i + 1) % count) for i in range(ends)]),
                cells,
                lax.ppermute(head, axis, [((i + 1) % count, i) for i in range(ends)]),
            ],
            axis=dim,
        )
    return cells


def coefficient_maps(wind_x, wind_y, patch_map, kappa_table):
    labels = jnp.arange(PATCHES, dtype=jnp.int32)
    member = (patch_map[:, :, None] == labels).astype(jnp.float32)
    diffusivity = jnp.sum(member * kappa_table, axis=-1)
    return (
        1.0 - 4.0 * diffusivity,
        diffusivity - 0.5 * wind_x,
        diffusivity + 0.5 * wind_x,
        diffusivity - 0.5 * wind_y,
        diffusivity + 0.5 * wind_y,
    )


def step_lead(current, weights):
    middle = current[1:-1]
    padded = jnp.pad(middle, ((0, 0), (1, 1), (0, 0)))
    centre, north, south, east, west = [weight[1:-1, :, None] for weight in weights]
    return (
        centre * middle
        + north * current[2:]
        + south * current[:-2]
        + east * padded[:, 2:]
        + west * padded[:, :-2]
    )


def step_middle(current, weights):
    middle = current[:, 1:-1]
    padded = jnp.pad(middle, ((0, 0), (0, 0), (1, 1)))
    centre, north, south, east, west = [weight[1:-1] for weight in weights]
    return (
        centre * middle
        + north * current[:, 2:]
        + south * current[:, :-2]
        + east * padded[:, :, 2:]
        + west * padded[:, :, :-2]
    )


def per_device(covariance, wind_x, wind_y, patch_map, kappa_table):
    weights = coefficient_maps(wind_x, wind_y, patch_map, kappa_table)
    bordered = tuple((jnp.pad(weight, ((2, 2), (0, 0))) for weight in weights))
    row_count, col_count = covariance.shape
    slab_rows = row_count // GY
    row_first = lax.axis_index("row") * slab_rows
    local_row = tuple(
        (lax.dynamic_slice_in_dim(weight, row_first, slab_rows + 4, 0) for weight in bordered)
    )
    inner_row = tuple((weight[1:-1] for weight in local_row))
    current = covariance.reshape(slab_rows, GY, col_count)
    for _ in range(SUBSTEPS // 2):
        widened = with_halo(current, (("row", 0),), 2)
        current = step_lead(step_lead(widened, local_row), inner_row)
    propagated = current.reshape(row_count, col_count)
    slab_cols = col_count // GY
    col_first = lax.axis_index("col") * slab_cols
    local_col = tuple(
        (lax.dynamic_slice_in_dim(weight, col_first, slab_cols + 4, 0) for weight in bordered)
    )
    inner_col = tuple((weight[1:-1] for weight in local_col))
    current = propagated.reshape(row_count, slab_cols, GY)
    for _ in range(SUBSTEPS // 2):
        widened = with_halo(current, (("col", 1),), 2)
        current = step_middle(step_middle(widened, local_col), inner_col)
    return current.reshape(row_count, col_count)


def solution(mesh):
    return jax.shard_map(
        per_device,
        mesh=mesh,
        in_specs=(P("row", "col"), P(), P(), P(), P()),
        out_specs=P("row", "col"),
        check_vma=False,
    )
```

profile of v0, /device:TPU:232, one launch (start us, length us, event | category | flops | bytes accessed | tf_op | source)
XLA Modules:
  0.0 220.5 jit_solution(15766750263453922217)
XLA Ops:
  0.0 2.7 %fusion.51 = (f32[256,1024]{1,0:T(8,128)S(1)}, f32[256,1024]{1,0:T(8,128)}) fusion(f32[1024,1024]{1,0:T(8,128)} %param.5), kind=kLoop, calls=%fused_computation.119 | loop fusion | bytes 4194304 | tf_op jit(solution)/shard_map/slice | solution.py:16
  2.7 5.0 %collective-permute-start.1 = (f32[2,128,1024]{2,1,0:T(8,128)}, f32[2,128,1024]{2,1,0:T(8,128)S(1)}, u32[]{:S(2)}, u32[]{:S(2)}) collective-permute-start(f32[2,128,1024]{2,1,0:T(8,128)} %bitcast.2), channel_id=1, source_target_pairs={{16,0},{32,16},{48,32},{64,48},{80,64},{96,80},{112,96},{128,112},... | collective-permute-start | bytes 3145736 | tf_op jit(solution)/shard_map/ppermute | solution.py:21
  7.7 1.9 collective-permute-start
  9.6 1.3 select_reduce_fusion
  10.9 0.9 multiply_subtract_fusion.2
  12.0 8.3 %collective-permute-done.1 = f32[2,128,1024]{2,1,0:T(8,128)S(1)} collective-permute-done((f32[2,128,1024]{2,1,0:T(8,128)}, f32[2,128,1024]{2,1,0:T(8,128)S(1)}, u32[]{:S(2)}, u32[]{:S(2)}) %collective-permute-start.1) | collective-permute-done | bytes 1048608 | tf_op jit(solution)/shard_map/ppermute | solution.py:21
  20.3 9.7 %collective-permute-done = f32[2,128,1024]{2,1,0:T(8,128)} collective-permute-done((f32[2,128,1024]{2,1,0:T(8,128)S(1)}, f32[2,128,1024]{2,1,0:T(8,128)}, u32[]{:S(2)}, u32[]{:S(2)}) %collective-permute-start) | collective-permute-done | bytes 1048608 | tf_op jit(solution)/shard_map/ppermute | solution.py:19
  30.0 0.0 copy-start
  30.0 3.1 %pad_maximum_fusion.6 = f32[10,128,1024]{2,1,0:T(8,128)S(1)} fusion(f32[2,128,1024]{2,1,0:T(8,128)S(1)} %collective-permute-done.1, f32[8,128,1024]{2,1,0:T(8,128)} %bitcast.13, f32[2,128,1024]{2,1,0:T(8,128)} %collective-permute-done), kind=kLoop, calls=%fused_computation.42 | loop fusion | flops 2621440 | bytes 11534336 | tf_op jit(solution)/shard_map/concatenate | solution.py:17
  33.2 0.5 copy-done
  33.6 4.2 %fusion.14 = f32[10,128,1024]{2,1,0:T(8,128)S(1)} fusion(f32[10,128,1024]{2,1,0:T(8,128)S(1)} %pad_maximum_fusion.6, f32[2,128,1024]{2,1,0:T(8,128)S(1)} %collective-permute-done.1, f32[8,128,1024]{2,1,0:T(8,128)S(1)} %bitcast.14, f32[2,128,1024]{2,1,0:T(8,128)} %collective-permute-done, f32[10,128]{1,0:T(8,128)S(1)} %get-tuple-element.36, ...), kind=kLoop, calls=%fused_computation.34 | loop fusion | flops 14417920 | bytes 16802816 | tf_op jit(solution)/shard_map/add | solution.py:46
  37.8 0.3 slice.304
  38.1 2.3 %fusion.26 = f32[8,128,1024]{2,1,0:T(8,128)S(1)} fusion(f32[8,128,1024]{2,1,0:T(8,128)S(1)} %slice.304, f32[10,128,1024]{2,1,0:T(8,128)S(1)} %fusion.14, f32[8,128]{1,0:T(8,128)S(1)} %get-tuple-element.26, f32[8,128]{1,0:T(8,128)S(1)} %get-tuple-element.45, f32[8,128]{1,0:T(8,128)S(1)} %get-tuple-element.22, f32[8,128]{1,0:T(8,128)S(1)} %get-tuple-element.47, ...), kind=kLoop, calls=%fused_computation.58 | loop fusion | flops 9437184 | bytes 16797696 | tf_op jit(solution)/shard_map/add | solution.py:46
  40.4 0.2 fusion.50
  40.6 1.9 collective-permute-start.2
  42.6 9.7 %collective-permute-start.3 = (f32[2,128,1024]{2,1,0:T(8,128)S(1)}, f32[2,128,1024]{2,1,0:T(8,128)}, u32[]{:S(2)}, u32[]{:S(2)}) collective-permute-start(f32[2,128,1024]{2,1,0:T(8,128)S(1)} %get-tuple-element.10), channel_id=1, source_target_pairs={{16,0},{32,16},{48,32},{64,48},{80,64},{96,80},{112,96},{128,112},... | collective-permute-start | bytes 3145736 | tf_op jit(solution)/shard_map/ppermute | solution.py:21
  52.2 10.6 %collective-permute-done.2 = f32[2,128,1024]{2,1,0:T(8,128)S(1)} collective-permute-done((f32[2,128,1024]{2,1,0:T(8,128)S(1)}, f32[2,128,1024]{2,1,0:T(8,128)S(1)}, u32[]{:S(2)}, u32[]{:S(2)}) %collective-permute-start.2) | collective-permute-done | bytes 1048608 | tf_op jit(solution)/shard_map/ppermute | solution.py:19
  62.9 1.7 collective-permute-done.3
  64.5 1.9 pad_maximum_fusion.4
  66.4 4.2 %fusion.18 = f32[10,128,1024]{2,1,0:T(8,128)S(1)} fusion(f32[10,128,1024]{2,1,0:T(8,128)S(1)} %pad_maximum_fusion.4, f32[2,128,1024]{2,1,0:T(8,128)} %collective-permute-done.3, f32[8,128,1024]{2,1,0:T(8,128)S(1)} %fusion.26, f32[2,128,1024]{2,1,0:T(8,128)S(1)} %collective-permute-done.2, f32[10,128]{1,0:T(8,128)S(1)} %get-tuple-element.36, ...), kind=kLoop, calls=%fused_computation.38 | loop fusion | flops 14417920 | bytes 16802816 | tf_op jit(solution)/shard_map/add | solution.py:46
  70.6 0.3 slice.309
  70.9 2.3 %fusion.30 = f32[8,128,1024]{2,1,0:T(8,128)S(1)} fusion(f32[8,128,1024]{2,1,0:T(8,128)S(1)} %slice.309, f32[10,128,1024]{2,1,0:T(8,128)S(1)} %fusion.18, f32[8,128]{1,0:T(8,128)S(1)} %get-tuple-element.26, f32[8,128]{1,0:T(8,128)S(1)} %get-tuple-element.45, f32[8,128]{1,0:T(8,128)S(1)} %get-tuple-element.22, f32[8,128]{1,0:T(8,128)S(1)} %get-tuple-element.47, ...), kind=kLoop, calls=%fused_computation.62 | loop fusion | flops 9437184 | bytes 16797696 | tf_op jit(solution)/shard_map/add | solution.py:46
  73.2 1.0 copy.6
  74.2 0.6 fusion.49
  74.9 2.1 collective-permute-start.4
  77.0 16.9 %collective-permute-start.5 = (f32[1024,2,128]{2,1,0:T(2,128)S(1)}, f32[1024,2,128]{2,1,0:T(2,128)S(1)}, u32[]{:S(2)}, u32[]{:S(2)}) collective-permute-start(f32[1024,2,128]{2,1,0:T(2,128)S(1)} %get-tuple-element.8), channel_id=1, source_target_pairs={{1,0},{2,1},{3,2},{4,3},{5,4},{6,5},{7,6},{8,7},{9,8},{10,9},{11,1... | collective-permute-start | bytes 3145736 | tf_op jit(solution)/shard_map/ppermute | solution.py:21
  93.9 15.2 %collective-permute-done.4 = f32[1024,2,128]{2,1,0:T(2,128)S(1)} collective-permute-done((f32[1024,2,128]{2,1,0:T(2,128)S(1)}, f32[1024,2,128]{2,1,0:T(2,128)S(1)}, u32[]{:S(2)}, u32[]{:S(2)}) %collective-permute-start.4) | collective-permute-done | bytes 1048608 | tf_op jit(solution)/shard_map/ppermute | solution.py:19
  109.1 60.8 %collective-permute-done.5 = f32[1024,2,128]{2,1,0:T(2,128)S(1)} collective-permute-done((f32[1024,2,128]{2,1,0:T(2,128)S(1)}, f32[1024,2,128]{2,1,0:T(2,128)S(1)}, u32[]{:S(2)}, u32[]{:S(2)}) %collective-permute-start.5) | collective-permute-done | bytes 1048608 | tf_op jit(solution)/shard_map/ppermute | solution.py:21
  169.9 1.8 pad_maximum_fusion.2
  171.7 4.9 %fusion.2 = f32[1024,10,128]{2,1,0:T(8,128)S(1)} fusion(f32[1024,10,128]{2,1,0:T(8,128)S(1)} %pad_maximum_fusion.2, f32[1024,2,128]{2,1,0:T(2,128)S(1)} %collective-permute-done.5, f32[1024,8,128]{2,1,0:T(8,128)S(1)} %bitcast.12, f32[1024,2,128]{2,1,0:T(2,128)S(1)} %collective-permute-done.4, f32[10,128]{1,0:T(8,128)S(1)} %get-tuple-element.35, ...), kind=kLoop, calls=%fused_computation.10 | loop fusion | flops 14417920 | bytes 16802816 | tf_op jit(solution)/shard_map/add | solution.py:59
  176.6 0.4 slice.314
  177.0 2.4 %fusion.34 = f32[1024,8,128]{2,1,0:T(8,128)S(1)} fusion(f32[1024,8,128]{2,1,0:T(8,128)S(1)} %slice.314, f32[1024,10,128]{2,1,0:T(8,128)S(1)} %fusion.2, f32[8,128]{1,0:T(8,128)S(1)} %get-tuple-element.25, f32[8,128]{1,0:T(8,128)S(1)} %get-tuple-element.46, f32[8,128]{1,0:T(8,128)S(1)} %get-tuple-element.21, f32[8,128]{1,0:T(8,128)S(1)} %get-tuple-element.48, ...), kind=kLoop, calls=%fused_computation.66 | loop fusion | flops 9437184 | bytes 16797696 | tf_op jit(solution)/shard_map/add | solution.py:59
  179.4 0.6 fusion.48
  180.0 1.9 collective-permute-start.6
  181.9 3.9 %collective-permute-start.7 = (f32[1024,2,128]{2,1,0:T(2,128)S(1)}, f32[1024,2,128]{2,1,0:T(2,128)S(1)}, u32[]{:S(2)}, u32[]{:S(2)}) collective-permute-start(f32[1024,2,128]{2,1,0:T(2,128)S(1)} %get-tuple-element.6), channel_id=1, source_target_pairs={{1,0},{2,1},{3,2},{4,3},{5,4},{6,5},{7,6},{8,7},{9,8},{10,9},{11,1... | collective-permute-start | bytes 3145736 | tf_op jit(solution)/shard_map/ppermute | solution.py:21
  185.9 22.1 %collective-permute-done.6 = f32[1024,2,128]{2,1,0:T(2,128)S(1)} collective-permute-done((f32[1024,2,128]{2,1,0:T(2,128)S(1)}, f32[1024,2,128]{2,1,0:T(2,128)S(1)}, u32[]{:S(2)}, u32[]{:S(2)}) %collective-permute-start.6) | collective-permute-done | bytes 1048608 | tf_op jit(solution)/shard_map/ppermute | solution.py:19
  207.9 0.0 collective-permute-done.7
  207.9 1.8 pad_maximum_fusion
  209.7 4.9 %fusion.6 = f32[1024,10,128]{2,1,0:T(8,128)S(1)} fusion(f32[1024,10,128]{2,1,0:T(8,128)S(1)} %pad_maximum_fusion, f32[1024,2,128]{2,1,0:T(2,128)S(1)} %collective-permute-done.7, f32[1024,8,128]{2,1,0:T(8,128)S(1)} %fusion.34, f32[1024,2,128]{2,1,0:T(2,128)S(1)} %collective-permute-done.6, f32[10,128]{1,0:T(8,128)S(1)} %get-tuple-element.35, ...), kind=kLoop, calls=%fused_computation.14 | loop fusion | flops 14417920 | bytes 16802816 | tf_op jit(solution)/shard_map/add | solution.py:59
  214.7 0.4 slice.319
  215.1 2.4 %fusion.38 = f32[1024,8,128]{2,1,0:T(8,128)S(1)} fusion(f32[1024,8,128]{2,1,0:T(8,128)S(1)} %slice.319, f32[1024,10,128]{2,1,0:T(8,128)S(1)} %fusion.6, f32[8,128]{1,0:T(8,128)S(1)} %get-tuple-element.25, f32[8,128]{1,0:T(8,128)S(1)} %get-tuple-element.46, f32[8,128]{1,0:T(8,128)S(1)} %get-tuple-element.21, f32[8,128]{1,0:T(8,128)S(1)} %get-tuple-element.48, ...), kind=kLoop, calls=%fused_computation.70 | loop fusion | flops 9437184 | bytes 16797696 | tf_op jit(solution)/shard_map/add | solution.py:59
  217.4 3.0 %copy.9 = f32[128,8,8,128]{3,1,2,0:T(8,128)} copy(f32[128,8,8,128]{3,2,1,0:T(8,128)S(1)} %bitcast.16) | data formatting | bytes 8388608
  (6 shorter events, 0.2 us)
Async XLA Ops:
  2.7 17.6 %collective-permute-start.1 = (f32[2,128,1024]{2,1,0:T(8,128)}, f32[2,128,1024]{2,1,0:T(8,128)S(1)}, u32[]{:S(2)}, u32[]{:S(2)}) collective-permute-start(f32[2,128,1024]{2,1,0:T(8,128)} %bitcast.2), channel_id=1, source_target_pairs={{16,0},{32,16},{48,32},{64,48},{80,64},{96,80},{112,96},{128,112},... | collective-permute-start | bytes 3145736 | tf_op jit(solution)/shard_map/ppermute | solution.py:21
  7.7 22.3 %collective-permute-start = (f32[2,128,1024]{2,1,0:T(8,128)S(1)}, f32[2,128,1024]{2,1,0:T(8,128)}, u32[]{:S(2)}, u32[]{:S(2)}) collective-permute-start(f32[2,128,1024]{2,1,0:T(8,128)S(1)} %bitcast.17), channel_id=1, source_target_pairs={{0,16},{16,32},{32,48},{48,64},{64,80},{80,96},{96,112},{112,128},... | collective-permute-start | bytes 3145736 | tf_op jit(solution)/shard_map/ppermute | solution.py:19
  30.0 3.6 %copy-start = (f32[1024,1024]{1,0:T(8,128)S(1)}, f32[1024,1024]{1,0:T(8,128)}, u32[]{:S(2)}) copy-start(f32[1024,1024]{1,0:T(8,128)} %param.5) | copy-start | bytes 12582916
  40.6 22.2 %collective-permute-start.2 = (f32[2,128,1024]{2,1,0:T(8,128)S(1)}, f32[2,128,1024]{2,1,0:T(8,128)S(1)}, u32[]{:S(2)}, u32[]{:S(2)}) collective-permute-start(f32[2,128,1024]{2,1,0:T(8,128)S(1)} %get-tuple-element.9), channel_id=1, source_target_pairs={{0,16},{16,32},{32,48},{48,64},{64,80},{80,96},{96,112},{112,128},... | collective-permute-start | bytes 3145736 | tf_op jit(solution)/shard_map/ppermute | solution.py:19
  42.6 22.0 %collective-permute-start.3 = (f32[2,128,1024]{2,1,0:T(8,128)S(1)}, f32[2,128,1024]{2,1,0:T(8,128)}, u32[]{:S(2)}, u32[]{:S(2)}) collective-permute-start(f32[2,128,1024]{2,1,0:T(8,128)S(1)} %get-tuple-element.10), channel_id=1, source_target_pairs={{16,0},{32,16},{48,32},{64,48},{80,64},{96,80},{112,96},{128,112},... | collective-permute-start | bytes 3145736 | tf_op jit(solution)/shard_map/ppermute | solution.py:21
  74.9 34.3 %collective-permute-start.4 = (f32[1024,2,128]{2,1,0:T(2,128)S(1)}, f32[1024,2,128]{2,1,0:T(2,128)S(1)}, u32[]{:S(2)}, u32[]{:S(2)}) collective-permute-start(f32[1024,2,128]{2,1,0:T(2,128)S(1)} %get-tuple-element.7), channel_id=1, source_target_pairs={{0,1},{1,2},{2,3},{3,4},{4,5},{5,6},{6,7},{7,8},{8,9},{9,10},{10,1... | collective-permute-start | bytes 3145736 | tf_op jit(solution)/shard_map/ppermute | solution.py:19
  77.0 92.9 %collective-permute-start.5 = (f32[1024,2,128]{2,1,0:T(2,128)S(1)}, f32[1024,2,128]{2,1,0:T(2,128)S(1)}, u32[]{:S(2)}, u32[]{:S(2)}) collective-permute-start(f32[1024,2,128]{2,1,0:T(2,128)S(1)} %get-tuple-element.8), channel_id=1, source_target_pairs={{1,0},{2,1},{3,2},{4,3},{5,4},{6,5},{7,6},{8,7},{9,8},{10,9},{11,1... | collective-permute-start | bytes 3145736 | tf_op jit(solution)/shard_map/ppermute | solution.py:21
  180.0 27.9 %collective-permute-start.6 = (f32[1024,2,128]{2,1,0:T(2,128)S(1)}, f32[1024,2,128]{2,1,0:T(2,128)S(1)}, u32[]{:S(2)}, u32[]{:S(2)}) collective-permute-start(f32[1024,2,128]{2,1,0:T(2,128)S(1)} %get-tuple-element.5), channel_id=1, source_target_pairs={{0,1},{1,2},{2,3},{3,4},{4,5},{5,6},{6,7},{7,8},{8,9},{9,10},{10,1... | collective-permute-start | bytes 3145736 | tf_op jit(solution)/shard_map/ppermute | solution.py:19
  181.9 26.0 %collective-permute-start.7 = (f32[1024,2,128]{2,1,0:T(2,128)S(1)}, f32[1024,2,128]{2,1,0:T(2,128)S(1)}, u32[]{:S(2)}, u32[]{:S(2)}) collective-permute-start(f32[1024,2,128]{2,1,0:T(2,128)S(1)} %get-tuple-element.6), channel_id=1, source_target_pairs={{1,0},{2,1},{3,2},{4,3},{5,4},{6,5},{7,6},{8,7},{9,8},{10,9},{11,1... | collective-permute-start | bytes 3145736 | tf_op jit(solution)/shard_map/ppermute | solution.py:21
where the time goes:
time: 221 us; the launch traced here: 220 us
  waiting for transfers between devices  128 us (58%)
  starting transfers between devices  43.4 us (20%)
  other arithmetic  38.2 us (17%)
  local copies, waits for them, and re-layouts  10.3 us (5%)
    ppermute x4, waiting for transfers between devices, with_halo(): lax.ppermute(head, axis, [((i + 1) % count, i) for i in range(ends)])  70.7 us
    ppermute x4, waiting for transfers between devices, with_halo(): lax.ppermute(tail, axis, [(i, (i + 1) % count) for i in range(ends)])  57.6 us
    ppermute x4, starting transfers between devices, with_halo(): lax.ppermute(head, axis, [((i + 1) % count, i) for i in range(ends)])  35.5 us
    add x4, other arithmetic, step_middle(): centre * middle + north * current[:, 2:] + south * current[:, :-2]  14.5 us
    add x4, other arithmetic, step_lead(): centre * middle + north * current[2:] + south * current[:-2]  12.9 us
    concatenate x4, other arithmetic, with_halo(): jnp.concatenate([lax.ppermute(tail, axis, [(i, (i + 1) % count) for i in...  8.59 us
    ppermute x4, starting transfers between devices, with_halo(): lax.ppermute(tail, axis, [(i, (i + 1) % count) for i in range(ends)])  7.88 us
    unnamed x4, local copies, waits for them, and re-layouts  4.48 us
  transfers between devices with their start and end apart: 8, of which 7 were waited for; matrix products, arithmetic and copies ran while one was open for 1% of the time, Pallas kernels for 0%

commit v1 on v0

v1 whole, which is shorter than its diff:
```python
import jax
import jax.numpy as jnp
from jax import lax
from jax.experimental import pallas as pl
from jax.experimental.pallas import tpu as pltpu
from jax.sharding import PartitionSpec as P

GY = 128
PATCHES = 16
MESH = pl.DeviceIdType.MESH
ORDER = (0, 7, 1, 6, 2, 5, 3, 4)
HALF = 512


def coefficients(wind_x, wind_y, patch_map, kappa_table):
    kappa = jnp.zeros((GY, GY), jnp.float32)
    for label in range(PATCHES):
        kappa = jnp.where(patch_map[...] == label, kappa_table[label], kappa)
    y = lax.broadcasted_iota(jnp.int32, (GY, GY), 1)
    half_x, half_y = 0.5 * wind_x[...], 0.5 * wind_y[...]
    return (
        1.0 - 4.0 * kappa,
        kappa - half_x,
        kappa + half_x,
        jnp.where(y < GY - 1, kappa - half_y, 0.0),
        jnp.where(y > 0, kappa + half_y, 0.0),
    )


def kernel(
    cov, wind_x, wind_y, patch_map, kappa_table, out,
    wide, f0, f1, f2, f3, final, lane_coef, sub_coef, padded,
    own_sem, out_sem, col_send, col_recv, row_send, row_recv,
):
    r, c = lax.axis_index("row"), lax.axis_index("col")
    rows, cols = lax.axis_size("row"), lax.axis_size("col")
    has = {"up": r > 0, "down": r < rows - 1, "left": c > 0, "right": c < cols - 1}
    where = {"up": (r - 1, c), "down": (r + 1, c), "left": (r, c - 1), "right": (r, c + 1)}

    own = [
        pltpu.make_async_copy(
            cov.at[pl.ds(k * GY, GY), :], wide.at[pl.ds(k * GY, GY), pl.ds(HALF, 1024)], own_sem.at[k]
        )
        for k in range(8)
    ]
    for k in ORDER:
        own[k].start()

    barrier = pltpu.get_barrier_semaphore()
    for side in has:
        @pl.when(has[side])
        def _():
            pl.semaphore_signal(barrier, inc=1, device_id=where[side], device_id_type=MESH)
    pl.semaphore_wait(barrier, sum(there.astype(jnp.int32) for there in has.values()))

    def col_copy(side, k):
        i = 0 if side == "left" else 1
        return pltpu.make_async_remote_copy(
            src_ref=cov.at[pl.ds(k * GY, GY), pl.ds(HALF * i, HALF)],
            dst_ref=wide.at[pl.ds(k * GY, GY), pl.ds(1536 if i == 0 else 0, HALF)],
            send_sem=col_send.at[i, k],
            recv_sem=col_recv.at[i, k],
            device_id=where[side],
            device_id_type=MESH,
        )

    def row_copy(k):
        side = "up" if k < 4 else "down"
        return pltpu.make_async_remote_copy(
            src_ref=f0.at[4 + k],
            dst_ref=f0.at[12 + k if k < 4 else k - 4],
            send_sem=row_send.at[k],
            recv_sem=row_recv.at[k],
            device_id=where[side],
            device_id_type=MESH,
        )

    for k in ORDER:
        for side in ("left", "right"):
            @pl.when(has[side])
            def _():
                col_copy(side, k).start()

    maps = coefficients(wind_x, wind_y, patch_map, kappa_table)
    padded[...] = jnp.zeros_like(padded)
    for j in range(5):
        padded[j, pl.ds(8, GY), :] = maps[j]
    for j in range(5):
        window = padded[j, pl.ds(pl.multiple_of(8 * c, 8), 24), :]
        for w in range(14):
            lane_coef[j, w] = jnp.broadcast_to(window[5 + w : 6 + w, :], (8, GY))
    for j in range(5):
        turned = pltpu.roll(maps[j].T, lax.rem(132 - 8 * r, 128), 1)
        for w in range(14):
            place = 8 * r - 3 + w
            inside = jnp.logical_and(place >= 0, place < GY)
            column = jnp.broadcast_to(turned[:, w + 1 : w + 2], (GY, GY))
            sub_coef[w, j] = jnp.where(inside, column, 0.0)

    @pl.when(c == 0)
    def _():
        wide[:, pl.ds(0, HALF)] = jnp.zeros((1024, HALF), jnp.float32)

    @pl.when(c == cols - 1)
    def _():
        wide[:, pl.ds(1536, HALF)] = jnp.zeros((1024, HALF), jnp.float32)

    @pl.when(r == 0)
    def _():
        f0[pl.ds(0, 4)] = jnp.zeros((4, GY, 1024), jnp.float32)

    @pl.when(r == rows - 1)
    def _():
        f0[pl.ds(12, 4)] = jnp.zeros((4, GY, 1024), jnp.float32)

    def col_phase(k):
        def group(i, carry):
            base = pl.multiple_of(k * GY + i * 16, 16)
            inner = pl.multiple_of(i * 16, 16)
            slabs = [
                [wide[pl.ds(base + 8 * u, 8), pl.ds(GY * w, GY)] for u in range(2)] for w in range(16)
            ]
            for s in range(4):
                fresh = [None] * 16
                for w in range(s + 1, 15 - s):
                    cc, cn, cs, ce, cw = [lane_coef[j, w - 1] for j in range(5)]
                    fresh[w] = [
                        cc * slabs[w][u]
                        + cn * slabs[w + 1][u]
                        + cs * slabs[w - 1][u]
                        + ce * pltpu.roll(slabs[w][u], GY - 1, 1)
                        + cw * pltpu.roll(slabs[w][u], 1, 1)
                        for u in range(2)
                    ]
                slabs = fresh
            for w in range(4, 12):
                for u in range(2):
                    f0[4 + k, pl.ds(inner + 8 * u, 8), pl.ds(GY * (w - 4), GY)] = slabs[w][u]
            return carry

        lax.fori_loop(0, 8, group, 0)

    sub = lax.broadcasted_iota(jnp.int32, (8, GY), 0)

    def row_task(source, target, shift, g):
        def part(q, carry):
            lanes = [pl.ds(pl.multiple_of(q * 256 + GY * u, GY), GY) for u in range(2)]

            def load(grid, k, u):
                return source[grid, pl.ds(8 * k, 8), lanes[u]]

            here = [[load(g, 0, u) for u in range(2)]]
            ups = [[pltpu.roll(here[0][u], 7, 0) for u in range(2)]]
            last_down = [jnp.zeros((8, GY), jnp.float32)] * 2
            for k in range(16):
                if k < 15:
                    here.append([load(g, k + 1, u) for u in range(2)])
                    ups.append([pltpu.roll(here[k + 1][u], 7, 0) for u in range(2)])
                cc, cn, cs, ce, cw = [sub_coef[g - 1, j, pl.ds(8 * k, 8), :] for j in range(5)]
                for u in range(2):
                    down = pltpu.roll(here[k][u], 1, 0)
                    east = jnp.where(sub == 7, ups[k + 1][u], ups[k][u]) if k < 15 else ups[k][u]
                    west = jnp.where(sub == 0, last_down[u], down)
                    last_down[u] = down
                    target[g - shift, pl.ds(8 * k, 8), lanes[u]] = (
                        cc * here[k][u]
                        + cn * load(g + 1, k, u)
                        + cs * load(g - 1, k, u)
                        + ce * east
                        + cw * west
                    )
            return carry

        lax.fori_loop(0, 4, part, 0)

    for k in ORDER:
        own[k].wait()
        for side in ("left", "right"):
            source_side = "right" if side == "left" else "left"

            @pl.when(has[source_side])
            def _():
                col_copy(side, k).wait_recv()

        col_phase(k)

        @pl.when(has["up" if k < 4 else "down"])
        def _():
            row_copy(k).start()

    for k in ORDER:
        @pl.when(has["down" if k < 4 else "up"])
        def _():
            row_copy(k).wait_recv()

    fields = (f0, f1, f2, f3)
    for s in range(3):
        lax.fori_loop(s + 1, 15 - s, lambda g, x, s=s: row_task(fields[s], fields[s + 1], 0, g) or x, 0)

    def finish(g, carry):
        row_task(f3, final, 4, g)
        pltpu.make_async_copy(
            final.at[g - 4], out.at[pl.ds(pl.multiple_of((g - 4) * GY, GY), GY), :], out_sem.at[g - 4]
        ).start()
        return carry

    lax.fori_loop(4, 12, finish, 0)
    for k in range(8):
        pltpu.make_async_copy(final.at[k], out.at[pl.ds(k * GY, GY), :], out_sem.at[k]).wait()
        for side in ("left", "right"):
            @pl.when(has[side])
            def _():
                col_copy(side, k).wait_send()

        @pl.when(has["up" if k < 4 else "down"])
        def _():
            row_copy(k).wait_send()


def per_device(covariance, wind_x, wind_y, patch_map, kappa_table):
    f32 = jnp.float32
    dma = pltpu.SemaphoreType.DMA
    return pl.pallas_call(
        kernel,
        out_shape=jax.ShapeDtypeStruct(covariance.shape, f32),
        in_specs=[
            pl.BlockSpec(memory_space=pl.ANY),
            pl.BlockSpec(memory_space=pltpu.VMEM),
            pl.BlockSpec(memory_space=pltpu.VMEM),
            pl.BlockSpec(memory_space=pltpu.VMEM),
            pl.BlockSpec(memory_space=pltpu.SMEM),
        ],
        out_specs=pl.BlockSpec(memory_space=pl.ANY),
        scratch_shapes=[
            pltpu.VMEM((1024, 2048), f32),
            pltpu.VMEM((16, GY, 1024), f32),
            pltpu.VMEM((16, GY, 1024), f32),
            pltpu.VMEM((16, GY, 1024), f32),
            pltpu.VMEM((16, GY, 1024), f32),
            pltpu.VMEM((8, GY, 1024), f32),
            pltpu.VMEM((5, 14, 8, GY), f32),
            pltpu.VMEM((14, 5, GY, GY), f32),
            pltpu.VMEM((5, 144, GY), f32),
            dma((8,)),
            dma((8,)),
            dma((2, 8)),
            dma((2, 8)),
            dma((8,)),
            dma((8,)),
        ],
        compiler_params=pltpu.CompilerParams(
            collective_id=0, has_side_effects=True, vmem_limit_bytes=62 * 1024 * 1024
        ),
    )(covariance, wind_x, wind_y, patch_map, kappa_table)


def solution(mesh):
    return jax.shard_map(
        per_device,
        mesh=mesh,
        in_specs=(P("row", "col"), P(), P(), P(), P()),
        out_specs=P("row", "col"),
        check_vma=False,
    )
```

time: 221 us -> 166 us (0.75)
  the two profiles are of different devices: /device:TPU:232 before, /device:TPU:55 now
where the time goes in v1:
time: 166 us
  Pallas kernels  161 us (97%)
  local copies, waits for them, and re-layouts  4.79 us (3%)
    pallas_call x1, Pallas kernels, per_device(): pl.pallas_call(kernel, out_shape=jax.ShapeDtypeStruct(covariance.shape, f...  161 us
    unnamed x1, local copies, waits for them, and re-layouts  4.79 us

profile of v1, /device:TPU:55, one launch (start us, length us, event | category | flops | bytes accessed | tf_op | source)
XLA Modules:
  0.0 165.6 jit_solution(14055969736816111805)
XLA Ops:
  0.0 160.8 %shard_map.55 = f32[1024,1024]{1,0:T(8,128)} custom-call(f32[1024,1024]{1,0:T(8,128)} %cov.1, f32[128,128]{1,0:T(8,128)} %wind_x.1, f32[128,128]{1,0:T(8,128)} %wind_y.1, s32[128,128]{1,0:T(8,128)} %patch_map.1, f32[16]{0:T(128)} %kappa_table.1), custom_call_target="tpu_custom_call" | custom-call | tf_op jit(solution)/shard_map/pallas_call | solution.py:223
  160.9 4.8 %copy.7 = f32[1024,1024]{1,0:T(8,128)} copy(f32[1024,1024]{1,0:T(8,128)} %shard_map.55) | data formatting | bytes 8388608

commit v2 on v1

--- a/solution.py
+++ b/solution.py
@@ -8,7 +8,7 @@
 GY = 128
 PATCHES = 16
 MESH = pl.DeviceIdType.MESH
-ORDER = (0, 7, 1, 6, 2, 5, 3, 4)
+AHEAD = 2
 HALF = 512
 
 
@@ -29,57 +29,120 @@
 
 def kernel(
     cov, wind_x, wind_y, patch_map, kappa_table, out,
-    wide, f0, f1, f2, f3, final, lane_coef, sub_coef, padded,
-    own_sem, out_sem, col_send, col_recv, row_send, row_recv,
+    wide, f0, f1, f2, f3, final, relay, lane_coef, sub_coef, padded,
+    own_sem, out_sem, col_send, col_recv, far_send, far_recv, near_send, near_recv,
+    relay_send, relay_recv,
 ):
     r, c = lax.axis_index("row"), lax.axis_index("col")
     rows, cols = lax.axis_size("row"), lax.axis_size("col")
-    has = {"up": r > 0, "down": r < rows - 1, "left": c > 0, "right": c < cols - 1}
-    where = {"up": (r - 1, c), "down": (r + 1, c), "left": (r, c - 1), "right": (r, c + 1)}
-
-    own = [
-        pltpu.make_async_copy(
-            cov.at[pl.ds(k * GY, GY), :], wide.at[pl.ds(k * GY, GY), pl.ds(HALF, 1024)], own_sem.at[k]
-        )
-        for k in range(8)
-    ]
-    for k in ORDER:
-        own[k].start()
+    odd = lax.rem(r, 2)
+
+    def pick(even_value, odd_value):
+        return even_value + odd * (odd_value - even_value)
+
+    near_row, far_row = pick(r + 1, r - 1), pick(r - 1, r + 1)
+    has_far = jnp.logical_and(r > 0, r < rows - 1)
+    middle = jnp.logical_or(r == 7, r == 8)
+    direct = jnp.logical_and(has_far, jnp.logical_not(middle))
+    relay_col = 12 * lax.rem(c, 2) + lax.rem(c, 4)
+    sent_to = (9 * (r - 7) + 2 * (c // 4), relay_col)
+    taken_from = (9 * (8 - r) + 2 * (c // 4), relay_col)
+    is_relay = jnp.logical_and(c == relay_col, r // 8 == odd)
+    flow_col = 4 * (lax.rem(r, 8) // 2) + lax.rem(c, 4)
+    flow_from, flow_to = (7 + r // 8, flow_col), (8 - r // 8, flow_col)
+    has = {"left": c > 0, "right": c < cols - 1}
+    where = {"left": (r, c - 1), "right": (r, c + 1)}
+
+    def chunk(step):
+        return pick(step, 7 - step)
+
+    def chunk_rows(step):
+        return pl.ds(pl.multiple_of(chunk(step) * GY, GY), GY)
+
+    def own_copy(step):
+        return pltpu.make_async_copy(
+            cov.at[chunk_rows(step), :], wide.at[chunk_rows(step), pl.ds(HALF, 1024)], own_sem.at[step]
+        )
+
+    for step in range(8):
+        own_copy(step).start()
 
     barrier = pltpu.get_barrier_semaphore()
-    for side in has:
-        @pl.when(has[side])
+    peers = (
+        (has["left"], where["left"]),
+        (has["right"], where["right"]),
+        (r >= 0, (near_row, c)),
+        (direct, (far_row, c)),
+        (middle, sent_to),
+        (middle, taken_from),
+        (is_relay, flow_from),
+        (is_relay, flow_to),
+    )
+    for there, peer in peers:
+        @pl.when(there)
         def _():
-            pl.semaphore_signal(barrier, inc=1, device_id=where[side], device_id_type=MESH)
-    pl.semaphore_wait(barrier, sum(there.astype(jnp.int32) for there in has.values()))
-
-    def col_copy(side, k):
+            pl.semaphore_signal(barrier, inc=1, device_id=peer, device_id_type=MESH)
+    pl.semaphore_wait(barrier, sum(there.astype(jnp.int32) for there, _ in peers))
+
+    def col_copy(side, step):
         i = 0 if side == "left" else 1
         return pltpu.make_async_remote_copy(
-            src_ref=cov.at[pl.ds(k * GY, GY), pl.ds(HALF * i, HALF)],
-            dst_ref=wide.at[pl.ds(k * GY, GY), pl.ds(1536 if i == 0 else 0, HALF)],
-            send_sem=col_send.at[i, k],
-            recv_sem=col_recv.at[i, k],
+            src_ref=cov.at[chunk_rows(step), pl.ds(HALF * i, HALF)],
+            dst_ref=wide.at[chunk_rows(step), pl.ds(1536 if i == 0 else 0, HALF)],
+            send_sem=col_send.at[i, step],
+            recv_sem=col_recv.at[i, step],
             device_id=where[side],
             device_id_type=MESH,
         )
 
-    def row_copy(k):
-        side = "up" if k < 4 else "down"
-        return pltpu.make_async_remote_copy(
-            src_ref=f0.at[4 + k],
-            dst_ref=f0.at[12 + k if k < 4 else k - 4],
-            send_sem=row_send.at[k],
-            recv_sem=row_recv.at[k],
-            device_id=where[side],
-            device_id_type=MESH,
-        )
-
-    for k in ORDER:
+    def send_columns(step):
         for side in ("left", "right"):
             @pl.when(has[side])
             def _():
-                col_copy(side, k).start()
+                col_copy(side, step).start()
+
+    def far_copy(step):
+        return pltpu.make_async_remote_copy(
+            src_ref=f0.at[4 + chunk(step)],
+            dst_ref=f0.at[pick(12 + step, 3 - step)],
+            send_sem=far_send.at[step],
+            recv_sem=far_recv.at[step],
+            device_id=(far_row, c),
+            device_id_type=MESH,
+        )
+
+    def to_relay(step):
+        return pltpu.make_async_remote_copy(
+            src_ref=f0.at[4 + chunk(step)],
+            dst_ref=relay.at[step],
+            send_sem=far_send.at[step],
+            recv_sem=relay_recv.at[step],
+            device_id=sent_to,
+            device_id_type=MESH,
+        )
+
+    def from_relay(step):
+        return pltpu.make_async_remote_copy(
+            src_ref=relay.at[step],
+            dst_ref=f0.at[pick(3 - step, 12 + step)],
+            send_sem=relay_send.at[step],
+            recv_sem=far_recv.at[step],
+            device_id=flow_to,
+            device_id_type=MESH,
+        )
+
+    def near_copy(step):
+        return pltpu.make_async_remote_copy(
+            src_ref=f0.at[4 + chunk(step)],
+            dst_ref=f0.at[pick(step - 4, 19 - step)],
+            send_sem=near_send.at[step - 4],
+            recv_sem=near_recv.at[step - 4],
+            device_id=(near_row, c),
+            device_id_type=MESH,
+        )
+
+    for step in range(AHEAD):
+        send_columns(step)
 
     maps = coefficients(wind_x, wind_y, patch_map, kappa_table)
     padded[...] = jnp.zeros_like(padded)
@@ -113,7 +176,9 @@
     def _():
         f0[pl.ds(12, 4)] = jnp.zeros((4, GY, 1024), jnp.float32)
 
-    def col_phase(k):
+    def col_phase(step):
+        k = chunk(step)
+
         def group(i, carry):
             base = pl.multiple_of(k * GY + i * 16, 16)
             inner = pl.multiple_of(i * 16, 16)
@@ -173,48 +238,78 @@
 
         lax.fori_loop(0, 4, part, 0)
 
-    for k in ORDER:
-        own[k].wait()
-        for side in ("left", "right"):
-            source_side = "right" if side == "left" else "left"
-
-            @pl.when(has[source_side])
-            def _():
-                col_copy(side, k).wait_recv()
-
-        col_phase(k)
-
-        @pl.when(has["up" if k < 4 else "down"])
-        def _():
-            row_copy(k).start()
-
-    for k in ORDER:
-        @pl.when(has["down" if k < 4 else "up"])
-        def _():
-            row_copy(k).wait_recv()
-
-    fields = (f0, f1, f2, f3)
-    for s in range(3):
-        lax.fori_loop(s + 1, 15 - s, lambda g, x, s=s: row_task(fields[s], fields[s + 1], 0, g) or x, 0)
-
-    def finish(g, carry):
-        row_task(f3, final, 4, g)
-        pltpu.make_async_copy(
+    def out_copy(g):
+        return pltpu.make_async_copy(
             final.at[g - 4], out.at[pl.ds(pl.multiple_of((g - 4) * GY, GY), GY), :], out_sem.at[g - 4]
-        ).start()
-        return carry
-
-    lax.fori_loop(4, 12, finish, 0)
-    for k in range(8):
-        pltpu.make_async_copy(final.at[k], out.at[pl.ds(k * GY, GY), :], out_sem.at[k]).wait()
+        )
+
+    fields = (f0, f1, f2, f3, final)
+
+    def row_phase(first, last, slope):
+        for s in range(4):
+            def task(i, carry, s=s):
+                g = pick(i, 15 - i)
+                row_task(fields[s], fields[s + 1], 4 if s == 3 else 0, g)
+                if s == 3:
+                    out_copy(g).start()
+                return carry
+
+            lax.fori_loop(first + slope * s, last - s, task, 0)
+
+    for step in range(8):
+        if step + AHEAD < 8:
+            send_columns(step + AHEAD)
+        if step == 7:
+            @pl.when(has_far)
+            def _():
+                for i in range(4):
+                    far_copy(i).wait_recv()
+
+            row_phase(1, 10, 1)
+        own_copy(step).wait()
+        for side, other in (("left", "right"), ("right", "left")):
+            @pl.when(has[other])
+            def _():
+                col_copy(side, step).wait_recv()
+
+        col_phase(step)
+        if step < 4:
+            @pl.when(direct)
+            def _():
+                far_copy(step).start()
+
+            @pl.when(middle)
+            def _():
+                to_relay(step).start()
+        else:
+            near_copy(step).start()
+        if 1 <= step < 5:
+            @pl.when(is_relay)
+            def _():
+                to_relay(step - 1).wait_recv()
+                from_relay(step - 1).start()
+
+    for step in range(4, 8):
+        near_copy(step).wait_recv()
+    row_phase(10, 15, -1)
+
+    for step in range(8):
+        out_copy(4 + step).wait()
         for side in ("left", "right"):
             @pl.when(has[side])
             def _():
-                col_copy(side, k).wait_send()
-
-        @pl.when(has["up" if k < 4 else "down"])
-        def _():
-            row_copy(k).wait_send()
+                col_copy(side, step).wait_send()
+
+        if step < 4:
+            @pl.when(has_far)
+            def _():
+                far_copy(step).wait_send()
+
+            @pl.when(is_relay)
+            def _():
+                from_relay(step).wait_send()
+        else:
+            near_copy(step).wait_send()
 
 
 def per_device(covariance, wind_x, wind_y, patch_map, kappa_table):
@@ -238,6 +333,7 @@
             pltpu.VMEM((16, GY, 1024), f32),
             pltpu.VMEM((16, GY, 1024), f32),
             pltpu.VMEM((8, GY, 1024), f32),
+            pltpu.VMEM((4, GY, 1024), f32),
             pltpu.VMEM((5, 14, 8, GY), f32),
             pltpu.VMEM((14, 5, GY, GY), f32),
             pltpu.VMEM((5, 144, GY), f32),
@@ -245,8 +341,12 @@
             dma((8,)),
             dma((2, 8)),
             dma((2, 8)),
-            dma((8,)),
-            dma((8,)),
+            dma((4,)),
+            dma((4,)),
+            dma((4,)),
+            dma((4,)),
+            dma((4,)),
+            dma((4,)),
         ],
         compiler_params=pltpu.CompilerParams(
             collective_id=0, has_side_effects=True, vmem_limit_bytes=62 * 1024 * 1024

time: 166 us -> 144 us (0.87)
  the two profiles are of different devices: /device:TPU:55 before, /device:TPU:201 now
where the time goes in v2:
time: 144 us
  Pallas kernels  139 us (97%)
  local copies, waits for them, and re-layouts  4.79 us (3%)
    pallas_call x1, Pallas kernels, per_device(): pl.pallas_call(kernel, out_shape=jax.ShapeDtypeStruct(covariance.shape, f...  139 us
    unnamed x1, local copies, waits for them, and re-layouts  4.79 us

profile of v2, /device:TPU:201, one launch (start us, length us, event | category | flops | bytes accessed | tf_op | source)
XLA Modules:
  0.0 144.2 jit_solution(12623001477360826983)
XLA Ops:
  0.0 139.4 %shard_map.55 = f32[1024,1024]{1,0:T(8,128)} custom-call(f32[1024,1024]{1,0:T(8,128)} %cov.1, f32[128,128]{1,0:T(8,128)} %wind_x.1, f32[128,128]{1,0:T(8,128)} %wind_y.1, s32[128,128]{1,0:T(8,128)} %patch_map.1, f32[16]{0:T(128)} %kappa_table.1), custom_call_target="tpu_custom_call" | custom-call | tf_op jit(solution)/shard_map/pallas_call | solution.py:318
  139.4 4.8 %copy.7 = f32[1024,1024]{1,0:T(8,128)} copy(f32[1024,1024]{1,0:T(8,128)} %shard_map.55) | data formatting | bytes 8388608

commit v3 on v2

--- a/solution.py
+++ b/solution.py
@@ -43,13 +43,46 @@
     near_row, far_row = pick(r + 1, r - 1), pick(r - 1, r + 1)
     has_far = jnp.logical_and(r > 0, r < rows - 1)
     middle = jnp.logical_or(r == 7, r == 8)
-    direct = jnp.logical_and(has_far, jnp.logical_not(middle))
-    relay_col = 12 * lax.rem(c, 2) + lax.rem(c, 4)
-    sent_to = (9 * (r - 7) + 2 * (c // 4), relay_col)
-    taken_from = (9 * (8 - r) + 2 * (c // 4), relay_col)
-    is_relay = jnp.logical_and(c == relay_col, r // 8 == odd)
-    flow_col = 4 * (lax.rem(r, 8) // 2) + lax.rem(c, 4)
-    flow_from, flow_to = (7 + r // 8, flow_col), (8 - r // 8, flow_col)
+    grid_y, place = c // 4, lax.rem(c, 4)
+    even = lax.rem(c, 2) == 0
+    inner = jnp.logical_or(grid_y == 1, grid_y == 2)
+    outer = jnp.logical_or(
+        jnp.logical_and(grid_y == 0, even), jnp.logical_and(grid_y == 3, jnp.logical_not(even))
+    )
+
+    def straight(upward):
+        return jnp.logical_or(outer, jnp.logical_and(inner, place // 2 == upward))
+
+    opposite = jnp.where(inner, c, 4 * (3 - grid_y) + place)
+    sends_straight, takes_straight = straight(r - 7), straight(8 - r)
+    both, no = jnp.logical_and, jnp.logical_not
+    half = r // 8
+    outer_relay = both(no(has_far), jnp.logical_or(outer, both(inner, place // 2 != half)))
+    inner_relay = both(inner, r == 2 + 8 * half + 2 * (place // 2))
+    is_relay = jnp.logical_or(outer_relay, inner_relay)
+    flow_from, flow_to = (7 + half, opposite), (8 - half, opposite)
+    sent_to, taken_from = (15 * (r - 7), opposite), (15 * (8 - r), opposite)
+    inner_sent_to = (2 + 8 * (r - 7) + 2 * (place // 2), c)
+    inner_taken_from = (2 + 8 * (8 - r) + 2 * (place // 2), c)
+    split = both(middle, inner)
+
+    def direct(step):
+        straight_here = both(sends_straight, no(inner)) if step < 2 else sends_straight
+        return both(has_far, jnp.logical_or(no(middle), straight_here))
+
+    def relayed(step):
+        return both(middle, no(direct(step)))
+
+    def relays(step):
+        if step < 2:
+            return jnp.logical_or(inner_relay, both(outer_relay, no(inner)))
+        return outer_relay
+
+    def relay_for(step):
+        if step < 2:
+            return tuple(jnp.where(inner, x, y) for x, y in zip(inner_sent_to, sent_to))
+        return sent_to
+
     has = {"left": c > 0, "right": c < cols - 1}
     where = {"left": (r, c - 1), "right": (r, c + 1)}
 
@@ -72,9 +105,12 @@
         (has["left"], where["left"]),
         (has["right"], where["right"]),
         (r >= 0, (near_row, c)),
-        (direct, (far_row, c)),
-        (middle, sent_to),
-        (middle, taken_from),
+        (both(has_far, jnp.logical_or(no(middle), sends_straight)), (far_row, c)),
+        (both(middle, takes_straight), (far_row, c)),
+        (both(middle, no(sends_straight)), sent_to),
+        (both(middle, no(takes_straight)), taken_from),
+        (split, inner_sent_to),
+        (split, inner_taken_from),
         (is_relay, flow_from),
         (is_relay, flow_to),
     )
@@ -117,14 +153,14 @@
             dst_ref=relay.at[step],
             send_sem=far_send.at[step],
             recv_sem=relay_recv.at[step],
-            device_id=sent_to,
+            device_id=relay_for(step),
             device_id_type=MESH,
         )
 
     def from_relay(step):
         return pltpu.make_async_remote_copy(
             src_ref=relay.at[step],
-            dst_ref=f0.at[pick(3 - step, 12 + step)],
+            dst_ref=f0.at[3 - step + half * (9 + 2 * step)],
             send_sem=relay_send.at[step],
             recv_sem=far_recv.at[step],
             device_id=flow_to,
@@ -274,17 +310,17 @@
 
         col_phase(step)
         if step < 4:
-            @pl.when(direct)
+            @pl.when(direct(step))
             def _():
                 far_copy(step).start()
 
-            @pl.when(middle)
+            @pl.when(relayed(step))
             def _():
                 to_relay(step).start()
         else:
             near_copy(step).start()
         if 1 <= step < 5:
-            @pl.when(is_relay)
+            @pl.when(relays(step - 1))
             def _():
                 to_relay(step - 1).wait_recv()
                 from_relay(step - 1).start()
@@ -305,7 +341,7 @@
             def _():
                 far_copy(step).wait_send()
 
-            @pl.when(is_relay)
+            @pl.when(relays(step))
             def _():
                 from_relay(step).wait_send()
         else:

time: 144 us -> 133 us (0.924)
  the two profiles are of different devices: /device:TPU:201 before, /device:TPU:29 now
where the time goes in v3:
time: 133 us
  Pallas kernels  128 us (96%)
  local copies, waits for them, and re-layouts  4.79 us (4%)
    pallas_call x1, Pallas kernels, per_device(): pl.pallas_call(kernel, out_shape=jax.ShapeDtypeStruct(covariance.shape, f...  128 us
    unnamed x1, local copies, waits for them, and re-layouts  4.79 us

profile of v3, /device:TPU:29, one launch (start us, length us, event | category | flops | bytes accessed | tf_op | source)
XLA Modules:
  0.0 133.1 jit_solution(13828617422202401742)
XLA Ops:
  0.0 128.3 %shard_map.55 = f32[1024,1024]{1,0:T(8,128)} custom-call(f32[1024,1024]{1,0:T(8,128)} %cov.1, f32[128,128]{1,0:T(8,128)} %wind_x.1, f32[128,128]{1,0:T(8,128)} %wind_y.1, s32[128,128]{1,0:T(8,128)} %patch_map.1, f32[16]{0:T(128)} %kappa_table.1), custom_call_target="tpu_custom_call" | custom-call | tf_op jit(solution)/shard_map/pallas_call | solution.py:354
  128.3 4.8 %copy.7 = f32[1024,1024]{1,0:T(8,128)} copy(f32[1024,1024]{1,0:T(8,128)} %shard_map.55) | data formatting | bytes 8388608

commit v4 on v3

--- a/solution.py
+++ b/solution.py
@@ -348,10 +348,23 @@
             near_copy(step).wait_send()
 
 
+def hand_over(source, target, stage, read_sem, write_sem):
+    parts = [pl.ds(k * GY, GY) for k in range(8)]
+    reads = [pltpu.make_async_copy(source.at[p], stage.at[p], read_sem.at[k]) for k, p in enumerate(parts)]
+    writes = [pltpu.make_async_copy(stage.at[p], target.at[p], write_sem.at[k]) for k, p in enumerate(parts)]
+    for read in reads:
+        read.start()
+    for read, write in zip(reads, writes):
+        read.wait()
+        write.start()
+    for write in writes:
+        write.wait()
+
+
 def per_device(covariance, wind_x, wind_y, patch_map, kappa_table):
     f32 = jnp.float32
     dma = pltpu.SemaphoreType.DMA
-    return pl.pallas_call(
+    forecast = pl.pallas_call(
         kernel,
         out_shape=jax.ShapeDtypeStruct(covariance.shape, f32),
         in_specs=[
@@ -388,6 +401,13 @@
             collective_id=0, has_side_effects=True, vmem_limit_bytes=62 * 1024 * 1024
         ),
     )(covariance, wind_x, wind_y, patch_map, kappa_table)
+    return pl.pallas_call(
+        hand_over,
+        out_shape=jax.ShapeDtypeStruct(covariance.shape, f32),
+        in_specs=[pl.BlockSpec(memory_space=pl.ANY)],
+        out_specs=pl.BlockSpec(memory_space=pl.ANY),
+        scratch_shapes=[pltpu.VMEM((1024, 1024), f32), dma((8,)), dma((8,))],
+    )(forecast)
 
 
 def solution(mesh):

time: 133 us -> 132 us (level)
  local copies, waits for them, and re-layouts: 4.79 us -> 0 us
  Pallas kernels: 128 us -> 132 us
    unnamed x1 -> x0, local copies, waits for them, and re-layouts: 4.79 us -> none
    pallas_call x0 -> x1, Pallas kernels: none -> 3.58 us  [per_device(): pl.pallas_call(hand_over, out_shape=jax.ShapeDtypeStruct(covariance.shape...]
where the time goes in v4:
time: 132 us
  Pallas kernels  132 us (100%)
    pallas_call x1, Pallas kernels, per_device(): pl.pallas_call(kernel, out_shape=jax.ShapeDtypeStruct(covariance.shape, f...  128 us
    pallas_call x1, Pallas kernels, per_device(): pl.pallas_call(hand_over, out_shape=jax.ShapeDtypeStruct(covariance.shape...  3.58 us

profile of v4, /device:TPU:29, one launch (start us, length us, event | category | flops | bytes accessed | tf_op | source)
XLA Modules:
  0.0 131.9 jit_solution(11727578907189224621)
XLA Ops:
  0.0 128.3 %shard_map.55.source = f32[1024,1024]{1,0:T(8,128)} custom-call(f32[1024,1024]{1,0:T(8,128)} %cov.1, f32[128,128]{1,0:T(8,128)} %wind_x.1, f32[128,128]{1,0:T(8,128)} %wind_y.1, s32[128,128]{1,0:T(8,128)} %patch_map.1, f32[16]{0:T(128)} %kappa_table.1), custom_call_target="tpu_custom_call" | custom-call | tf_op jit(solution)/shard_map/pallas_call | solution.py:367
  128.3 3.6 %shard_map.56 = f32[1024,1024]{1,0:T(8,128)} custom-call(f32[1024,1024]{1,0:T(8,128)} %shard_map.55.source), custom_call_target="tpu_custom_call" | custom-call | tf_op jit(solution)/shard_map/pallas_call | solution.py:404
